TPU v7x, 32 devices: a whole 2x2x4 slice. The times are simulated.
32 devices in a mesh: gx: 4 (over x, core), gy: 4 (over z), gz: 2 (over y).
Axes of the slice: x: 2, y: 2, z: 4, core: 2. Of those that a mesh axis runs over, the one named last changes fastest.
Arguments:
- orbitals: float32 [16, 48, 48, 256], P(None, 'gx', 'gy', 'gz'), may hold values from -6 to 6
- potential: float32 [48, 48, 256], P('gx', 'gy', 'gz'), may hold values from 0 to 2
Outputs:
- filtered: float32 [16, 48, 48, 256], P(None, 'gx', 'gy', 'gz')
All inputs are finite; a program needn't handle non-finite values.
Results may differ from a plain program's by a relative error of at most 0.00002.
Values sent between devices are 32-bit elements; how exact they have to be, the bound alone decides.
A program may use at most 64 MiB of HBM per device.

v0:
```python
import jax
import jax.numpy as jnp
from jax import lax
from jax.sharding import PartitionSpec as P

DEGREE = 2


SECOND = (
    -5369.0 / 1800.0,
    12.0 / 7.0,
    -15.0 / 56.0,
    10.0 / 189.0,
    -1.0 / 112.0,
    2.0 / 1925.0,
    -1.0 / 16632.0,
)
FIRST = (6.0 / 7.0, -15.0 / 56.0, 5.0 / 63.0, -1.0 / 56.0, 3.0 / 385.0, -1.0 / 792.0)
METRIC = ((1.0, 0.25, 0.15), (0.25, 1.0, 0.2), (0.15, 0.2, 1.0))
CENTER = 10.5
HALF_WIDTH = 9.5


def extended(block, sides, width):
    for axis, dim in sides:
        count = lax.axis_size(axis)
        forward = [(i, i + 1) for i in range(count - 1)]
        forward.append((count - 1, 0))
        backward = [(target, source) for source, target in forward]
        low = lax.ppermute(
            lax.slice_in_dim(block, block.shape[dim] - width, None, axis=dim), axis, forward
        )
        high = lax.ppermute(lax.slice_in_dim(block, 0, width, axis=dim), axis, backward)
        block = jnp.concatenate([low, block, high], axis=dim)
    return block


def window(values, starts, lengths):
    leading = values.ndim - 3
    starts_full = (0,) * leading + tuple(starts)
    limits = tuple(values.shape[:leading]) + tuple((s + l for s, l in zip(starts, lengths)))
    return lax.slice(values, starts_full, limits)


def apply_operator(padded, potential):
    lengths = [padded.shape[i + 1] - 12 for i in range(3)]
    centre = window(padded, (6, 6, 6), lengths)
    summed = METRIC[0][0] * 0.0 * centre
    for d in range(3):
        second = SECOND[0] * centre
        for k in range(1, 7):
            forward = [6, 6, 6]
            forward[d] += k
            backward = [6, 6, 6]
            backward[d] -= k
            second = second + SECOND[k] * (
                window(padded, forward, lengths) + window(padded, backward, lengths)
            )
        summed = summed + METRIC[d][d] * second
    for d, e in ((0, 1), (0, 2), (1, 2)):
        widened = list(lengths)
        widened[d] += 12
        partial_sum = None
        for k in range(1, 7):
            forward = [6, 6, 6]
            forward[d] = 0
            forward[e] += k
            backward = [6, 6, 6]
            backward[d] = 0
            backward[e] -= k
            term = FIRST[k - 1] * (
                window(padded, forward, widened) - window(padded, backward, widened)
            )
            partial_sum = term if partial_sum is None else partial_sum + term
        crossed = None
        for k in range(1, 7):
            forward = [0, 0, 0]
            forward[d] = 6 + k
            backward = [0, 0, 0]
            backward[d] = 6 - k
            term = FIRST[k - 1] * (
                window(partial_sum, forward, lengths) - window(partial_sum, backward, lengths)
            )
            crossed = term if crossed is None else crossed + term
        summed = summed + 2.0 * METRIC[d][e] * crossed
    return -0.5 * summed + potential[None] * centre


def local(orbitals, potential):
    current = lax.all_to_all(
        lax.all_to_all(orbitals, "gx", split_axis=0, concat_axis=1, tiled=True),
        "gy",
        split_axis=0,
        concat_axis=2,
        tiled=True,
    )
    previous = jnp.zeros_like(current)
    plane_x = lax.all_gather(potential, "gx", axis=0, tiled=True)
    plane = lax.all_gather(plane_x, "gy", axis=1, tiled=True)
    for degree_step in range(DEGREE):
        slab = extended(current, (("gz", 3),), 6)
        padded = jnp.pad(slab, ((0, 0), (6, 6), (6, 6), (0, 0)), mode="wrap")
        applied = apply_operator(padded, plane)
        factor = 1.0 if degree_step == 0 else 2.0
        carry_factor = 0.0 if degree_step == 0 else 1.0
        following = factor * (applied - CENTER * current) / HALF_WIDTH - carry_factor * previous
        previous = current
        current = following
    partly = lax.all_to_all(current, "gy", split_axis=2, concat_axis=0, tiled=True)
    current = lax.all_to_all(partly, "gx", split_axis=1, concat_axis=0, tiled=True)
    return current


def solution(mesh):
    return jax.shard_map(
        local,
        mesh=mesh,
        in_specs=(P(None, "gx", "gy", "gz"), P("gx", "gy", "gz")),
        out_specs=P(None, "gx", "gy", "gz"),
        check_vma=False,
    )
```

profile of v0, /device:TPU:0, one launch (start us, length us, event | category | flops | bytes accessed | tf_op | source)
XLA Modules:
  0.0 310.5 jit_solution(17400182303846139604)
XLA Ops:
  6.5 0.0 all-gather.2.cloned.1.call-start
  6.5 1.7 copy.34
  8.2 24.1 %all_to_all.75 = f32[16,12,12,128]{3,2,1,0:T(8,128)S(1)} all-to-all(f32[16,12,12,128]{3,2,1,0:T(8,128)S(1)} %copy.34), channel_id=1, replica_groups=mesh['gx'=4,'gy'=4,'gz'=2] {'gx'}, dimensions={0} | all-to-all | bytes 2359296 | tf_op jit(solution)/shard_map/all_to_all | solution.py:91
  32.3 0.8 copy.35
  33.1 0.4 copy.36
  33.5 32.8 %all_to_all.76 = f32[4,48,12,128]{3,1,2,0:T(8,128)S(1)} all-to-all(f32[4,48,12,128]{3,1,2,0:T(8,128)S(1)} %copy.36), channel_id=1, replica_groups=mesh['gx'=4,'gy'=4,'gz'=2] {'gy'}, dimensions={0} | all-to-all | bytes 2359296 | tf_op jit(solution)/shard_map/all_to_all | solution.py:90
  66.3 1.4 fusion.266
  67.7 1.8 copy.37
  69.5 0.5 copy.38
  70.0 1.6 collective-permute-start.1
  71.6 0.5 collective-permute-start
  72.1 0.0 copy-done.13
  72.1 6.1 %all_gather.6 = f32[48,12,128]{2,1,0:T(8,128)S(1)} all-gather(f32[12,12,128]{2,1,0:T(8,128)S(1)} %copy-done.13), channel_id=1, replica_groups=mesh['gx'=4,'gy'=4,'gz'=2] {'gx'}, dimensions={0}, use_global_device_ids=true | all-gather | bytes 368640 | tf_op jit(solution)/shard_map/all_gather | solution.py:98
  78.2 0.8 copy.43
  79.1 0.0 all-gather.2.cloned.1.call-update
  79.1 0.0 collective-permute-done
  79.1 0.6 copy.39
  79.7 0.0 copy-start.7
  79.7 0.0 collective-permute-done.1
  79.7 1.6 copy.40
  81.3 1.5 pad_maximum_fusion.15
  82.8 0.0 copy-done.7
  82.8 0.0 copy-done.9
  82.8 1.2 pad_maximum_fusion.4
  84.0 0.1 fusion.264
  84.1 0.0 copy-start.12
  84.1 0.0 copy-start.8
  84.1 4.8 %fusion.23 = f32[1,60,48,128]{3,1,2,0:T(8,128)S(1)} fusion(f32[1,60,48,140]{3,1,2,0:T(8,128)S(1)} %pad_maximum_fusion.4), kind=kLoop, calls=%fused_computation.88 | loop fusion | flops 6266880 | bytes 19169280 | tf_op jit(solution)/shard_map/add | solution.py:74
  88.9 0.0 copy-done.12
  88.9 0.0 copy-done.8
  88.9 0.0 copy-start.10
  88.9 5.1 %pad_maximum_fusion.2 = (f32[1,60,54,140]{3,1,2,0:T(8,128)S(1)}, f32[1,60,54,140]{3,1,2,0:T(8,128)S(1)}) fusion(f32[1,60,6,140]{3,1,2,0:T(8,128)S(1)} %get-tuple-element.22, f32[1,6,48,140]{3,1,2,0:T(8,128)S(1)} %get-tuple-element.18, f32[1,48,48,6]{3,1,2,0:T(8,128)S(1)} %copy-done.9, f32[1,48,48,128]{3,1,2,0:T(8,128)S(1)} %bitcast.40, ...), kind=kLoop, calls=%fused_computation.42 | loop fusion | flops 4536000 | bytes 5644800 | tf_op jit(solution)/shard_map/jit(_pad)/concatenate | solution.py:102
  94.0 3.2 %pad_maximum_fusion = f32[1,60,60,140]{3,1,2,0:T(8,128)S(1)} fusion(f32[1,60,6,140]{3,1,2,0:T(8,128)} %copy-done.12, f32[1,6,48,140]{3,1,2,0:T(8,128)S(1)} %get-tuple-element.18, f32[1,48,48,6]{3,1,2,0:T(8,128)S(1)} %copy-done.10, f32[1,48,48,128]{3,1,2,0:T(8,128)S(1)} %bitcast.41, f32[1,48,48,6]{3,1,2,0:T(8,128)S(1)} %copy-done.8, ...), kind=kLoop, calls=%fused_computation.40 | loop fusion | flops 3024000 | bytes 4032000 | tf_op jit(solution)/shard_map/jit(_pad)/concatenate | solution.py:102
  97.2 4.5 %pad_maximum_fusion.6 = (f32[1,54,48,140]{3,1,2,0:T(8,128)}, f32[1,54,48,140]{3,1,2,0:T(8,128)}) fusion(f32[1,6,48,140]{3,1,2,0:T(8,128)S(1)} %get-tuple-element.18, f32[1,48,48,6]{3,1,2,0:T(8,128)S(1)} %copy-done.10, f32[1,48,48,128]{3,1,2,0:T(8,128)S(1)} %bitcast.42, f32[1,48,48,6]{3,1,2,0:T(8,128)S(1)} %copy-done.8, ...), kind=kLoop, calls=%fused_computation.48 | loop fusion | flops 2177280 | bytes 4515840 | tf_op jit(solution)/shard_map/jit(_pad)/concatenate | solution.py:102
  101.7 0.0 copy-done.3
  101.7 5.9 %fusion.34 = f32[1,60,48,128]{3,1,2,0:T(8,128)} fusion(f32[1,60,54,140]{3,1,2,0:T(8,128)S(1)} %get-tuple-element.10, f32[1,60,54,140]{3,1,2,0:T(8,128)S(1)} %get-tuple-element.9), kind=kLoop, calls=%fused_computation.105 | loop fusion | flops 6266880 | bytes 19169280 | tf_op jit(solution)/shard_map/add | solution.py:74
  107.6 4.5 %fusion.56 = f32[1,48,60,128]{3,1,2,0:T(8,128)S(1)} fusion(f32[1,60,60,140]{3,1,2,0:T(8,128)S(1)} %pad_maximum_fusion), kind=kLoop, calls=%fused_computation.139 | loop fusion | flops 6266880 | bytes 19169280 | tf_op jit(solution)/shard_map/add | solution.py:74
  112.1 0.0 all-gather.2.cloned.1.call-done
  112.2 52.2 %broadcast_multiply_fusion = (f32[1,48,48,128]{3,1,2,0:T(8,128)S(1)}, f32[1,48,48,128]{3,1,2,0:T(8,128)}) fusion(f32[1,48,48,128]{3,1,2,0:T(8,128)} %bitcast.43, f32[48,48,128]{2,0,1:T(8,128)} %all-gather.2.cloned.1.call-done, f32[4,48,12,128]{3,1,2,0:T(8,128)} %copy-done, f32[1,48,60,128]{3,1,2,0:T(8,128)S(1)} %fusion.56, ...), kind=kLoop, calls=%fused_computation.417 | loop fusion | flops 39518208 | bytes 76787712 | tf_op jit(solution)/shard_map/div | solution.py:106
  164.4 0.4 fusion.265
  164.8 0.6 copy-done.5
  165.4 0.5 copy.44
  165.9 1.6 collective-permute-start.2
  167.5 1.2 copy.45
  168.7 0.5 collective-permute-start.3
  169.2 3.4 %collective-permute-done.2 = f32[1,48,48,6]{2,1,3,0:T(8,128)S(1)} collective-permute-done((f32[1,48,48,6]{2,1,3,0:T(8,128)S(1)}, f32[1,48,48,6]{2,1,3,0:T(8,128)S(1)}, u32[]{:S(2)}, u32[]{:S(2)}) %collective-permute-start.2) | collective-permute-done | bytes 55328 | tf_op jit(solution)/shard_map/ppermute | solution.py:30
  172.6 0.6 copy.46
  173.2 2.0 collective-permute-done.3
  175.2 1.6 copy.47
  176.8 1.5 pad_maximum_fusion.12
  178.3 1.2 pad_maximum_fusion.5
  179.5 0.1 fusion.263
  179.6 5.0 %fusion.1 = f32[1,60,48,128]{3,1,2,0:T(8,128)S(1)} fusion(f32[1,60,48,140]{3,1,2,0:T(8,128)S(1)} %pad_maximum_fusion.5), kind=kLoop, calls=%fused_computation.54 | loop fusion | flops 6266880 | bytes 19169280 | tf_op jit(solution)/shard_map/add | solution.py:74
  184.6 4.4 %pad_maximum_fusion.7 = (f32[1,54,48,140]{3,1,2,0:T(8,128)}, f32[1,54,48,140]{3,1,2,0:T(8,128)}) fusion(f32[1,6,48,140]{3,1,2,0:T(8,128)S(1)} %get-tuple-element.14, f32[1,48,48,6]{3,1,2,0:T(8,128)S(1)} %copy-done.11, f32[1,48,48,128]{3,1,2,0:T(8,128)S(1)} %copy-done.6, f32[1,48,48,6]{3,1,2,0:T(8,128)S(1)} %copy.46, f32[1,6,48,140]{3,1,2,0:T(8,128)S(1)} %get-tuple-element.13), kind=kLoop, calls=%fused_computation.50 | loop fusion | flops 2177280 | bytes 4515840 | tf_op jit(solution)/shard_map/jit(_pad)/concatenate | solution.py:102
  189.0 3.1 %pad_maximum_fusion.1 = f32[1,60,60,140]{3,1,2,0:T(8,128)S(1)} fusion(f32[1,60,6,140]{3,1,2,0:T(8,128)S(1)} %get-tuple-element.20, f32[1,6,48,140]{3,1,2,0:T(8,128)S(1)} %get-tuple-element.14, f32[1,48,48,6]{3,1,2,0:T(8,128)S(1)} %copy-done.11, f32[1,48,48,128]{3,1,2,0:T(8,128)S(1)} %copy-done.6, f32[1,48,48,6]{3,1,2,0:T(8,128)S(1)} %copy.46, ...), kind=kLoop, calls=%fused_computation.41 | loop fusion | flops 3024000 | bytes 4032000 | tf_op jit(solution)/shard_map/jit(_pad)/concatenate | solution.py:102
  192.1 5.9 %pad_maximum_fusion.3 = (f32[1,60,54,140]{3,1,2,0:T(8,128)S(1)}, f32[1,60,54,140]{3,1,2,0:T(8,128)}) fusion(f32[1,60,6,140]{3,1,2,0:T(8,128)S(1)} %get-tuple-element.20, f32[1,6,48,140]{3,1,2,0:T(8,128)S(1)} %get-tuple-element.14, f32[1,48,48,6]{3,1,2,0:T(8,128)S(1)} %copy-done.11, f32[1,48,48,128]{3,1,2,0:T(8,128)S(1)} %copy-done.6, ...), kind=kLoop, calls=%fused_computation.44 | loop fusion | flops 4536000 | bytes 5644800 | tf_op jit(solution)/shard_map/jit(_pad)/concatenate | solution.py:102
  198.1 4.3 %fusion.45 = f32[1,48,60,128]{3,1,2,0:T(8,128)S(1)} fusion(f32[1,60,60,140]{3,1,2,0:T(8,128)S(1)} %pad_maximum_fusion.1), kind=kLoop, calls=%fused_computation.122 | loop fusion | flops 6266880 | bytes 19169280 | tf_op jit(solution)/shard_map/add | solution.py:74
  202.4 0.0 copy-start.1
  202.4 10.7 %fusion.12 = f32[1,60,48,128]{3,1,2,0:T(8,128)S(1)} fusion(f32[1,60,54,140]{3,1,2,0:T(8,128)} %get-tuple-element.8, f32[1,60,54,140]{3,1,2,0:T(8,128)S(1)} %get-tuple-element.7), kind=kLoop, calls=%fused_computation.71 | loop fusion | flops 6266880 | bytes 19169280 | tf_op jit(solution)/shard_map/add | solution.py:74
  213.2 37.9 %fusion.261 = f32[1,48,48,128]{3,1,0,2:T(8,128)} fusion(f32[1,48,48,128]{3,1,2,0:T(8,128)} %get-tuple-element.6, f32[1,48,48,128]{3,1,2,0:T(8,128)S(1)} %copy-done.6, f32[48,48,128]{2,0,1:T(8,128)} %all-gather.2.cloned.1.call-done, f32[1,48,60,128]{3,1,2,0:T(8,128)S(1)} %fusion.45, f32[1,60,48,128]{3,1,2,0:T(8,128)S(1)} %fusion.1, ...), kind=kLoop, calls=%fused_computation.416 | loop fusion | flops 39813120 | bytes 76787712 | tf_op jit(solution)/shard_map/sub | solution.py:106
  251.1 32.1 %all_to_all.77 = f32[1,48,48,128]{3,1,0,2:T(8,128)S(1)} all-to-all(f32[1,48,48,128]{3,1,0,2:T(8,128)} %fusion.261), channel_id=1, replica_groups=mesh['gx'=4,'gy'=4,'gz'=2] {'gy'}, dimensions={2} | all-to-all | bytes 2359296 | tf_op jit(solution)/shard_map/all_to_all | solution.py:109
  283.2 0.8 copy.51
  283.9 18.3 %all_to_all.78 = f32[4,48,12,128]{3,0,2,1:T(4,128)S(1)} all-to-all(f32[4,48,12,128]{3,0,2,1:T(4,128)S(1)} %copy.51), channel_id=1, replica_groups=mesh['gx'=4,'gy'=4,'gz'=2] {'gx'}, dimensions={1} | all-to-all | bytes 2359296 | tf_op jit(solution)/shard_map/all_to_all | solution.py:110
  302.2 1.3 copy.52
  (16 shorter events, 0.0 us)
Async XLA Ops:
  6.5 105.6 %all-gather.2.cloned.1.call-start = ((), (), s32[]{:S(2)}) async-start(), calls=%async_computation.4 | async-start | bytes 1474560 | tf_op jit(solution)/shard_map/all_gather | solution.py:99
  66.3 30.9 %copy-start = (f32[4,48,12,128]{3,1,2,0:T(8,128)}, f32[4,48,12,128]{3,1,2,0:T(8,128)S(1)}, u32[]{:S(2)}) copy-start(f32[4,48,12,128]{3,1,2,0:T(8,128)S(1)} %all_to_all.76) | copy-start | bytes 3538948
  67.7 4.4 %copy-start.13 = (f32[12,12,128]{2,1,0:T(8,128)S(1)}, f32[12,12,128]{2,1,0:T(8,128)}, u32[]{:S(2)}) copy-start(f32[12,12,128]{2,1,0:T(8,128)} %param.3) | copy-start | bytes 221188
  70.0 9.7 %collective-permute-start.1 = (f32[1,48,48,6]{2,1,3,0:T(8,128)S(1)}, f32[1,48,48,6]{2,1,3,0:T(8,128)S(1)}, u32[]{:S(2)}, u32[]{:S(2)}) collective-permute-start(f32[1,48,48,6]{2,1,3,0:T(8,128)S(1)} %copy.38), channel_id=1, source_target_pairs={{1,0},{0,1},{3,2},{2,3},{5,4},{4,5},{7,6},{6,7},{9,8},{8,9},{11,10... | collective-permute-start | bytes 165896 | tf_op jit(solution)/shard_map/ppermute | solution.py:33
  71.6 7.5 %collective-permute-start = (f32[1,48,48,6]{2,1,3,0:T(8,128)S(1)}, f32[1,48,48,6]{2,1,3,0:T(8,128)S(1)}, u32[]{:S(2)}, u32[]{:S(2)}) collective-permute-start(f32[1,48,48,6]{2,1,3,0:T(8,128)S(1)} %copy.37), channel_id=1, source_target_pairs={{0,1},{1,0},{2,3},{3,2},{4,5},{5,4},{6,7},{7,6},{8,9},{9,8},{10,11... | collective-permute-start | bytes 165896 | tf_op jit(solution)/shard_map/ppermute | solution.py:30
  79.7 3.1 copy-start.7
  81.3 1.5 copy-start.9
  84.1 4.8 %copy-start.12 = (f32[1,60,6,140]{3,1,2,0:T(8,128)}, f32[1,60,6,140]{3,1,2,0:T(8,128)S(1)}, u32[]{:S(2)}) copy-start(f32[1,60,6,140]{3,1,2,0:T(8,128)S(1)} %get-tuple-element.22) | copy-start | bytes 604804
  84.1 4.8 %copy-start.8 = (f32[1,48,48,6]{3,1,2,0:T(8,128)S(1)}, f32[1,48,48,6]{3,1,2,0:T(8,128)}, u32[]{:S(2)}) copy-start(f32[1,48,48,6]{3,1,2,0:T(8,128)} %copy-done.7) | copy-start | bytes 165892
  88.9 5.1 %copy-start.10 = (f32[1,48,48,6]{3,1,2,0:T(8,128)S(1)}, f32[1,48,48,6]{3,1,2,0:T(8,128)}, u32[]{:S(2)}) copy-start(f32[1,48,48,6]{3,1,2,0:T(8,128)} %copy.40) | copy-start | bytes 165892
  94.0 7.7 %copy-start.2 = (f32[1,60,54,140]{3,1,2,0:T(8,128)}, f32[1,60,54,140]{3,1,2,0:T(8,128)S(1)}, u32[]{:S(2)}) copy-start(f32[1,60,54,140]{3,1,2,0:T(8,128)S(1)} %get-tuple-element.9) | copy-start | bytes 5443204
  94.0 7.7 %copy-start.3 = (f32[1,60,54,140]{3,1,2,0:T(8,128)}, f32[1,60,54,140]{3,1,2,0:T(8,128)S(1)}, u32[]{:S(2)}) copy-start(f32[1,60,54,140]{3,1,2,0:T(8,128)S(1)} %get-tuple-element.10) | copy-start | bytes 5443204
  164.4 1.0 copy-start.5
  165.9 6.7 %collective-permute-start.2 = (f32[1,48,48,6]{2,1,3,0:T(8,128)S(1)}, f32[1,48,48,6]{2,1,3,0:T(8,128)S(1)}, u32[]{:S(2)}, u32[]{:S(2)}) collective-permute-start(f32[1,48,48,6]{2,1,3,0:T(8,128)S(1)} %copy.44), channel_id=1, source_target_pairs={{0,1},{1,0},{2,3},{3,2},{4,5},{5,4},{6,7},{7,6},{8,9},{9,8},{10,11... | collective-permute-start | bytes 165896 | tf_op jit(solution)/shard_map/ppermute | solution.py:30
  168.7 8.1 %copy-start.6 = (f32[1,48,48,128]{3,1,2,0:T(8,128)S(1)}, f32[1,48,48,128]{3,1,2,0:T(8,128)}, u32[]{:S(2)}) copy-start(f32[1,48,48,128]{3,1,2,0:T(8,128)} %copy-done.5) | copy-start | bytes 3538948
  168.7 6.5 %collective-permute-start.3 = (f32[1,48,48,6]{2,1,3,0:T(8,128)}, f32[1,48,48,6]{2,1,3,0:T(8,128)S(1)}, u32[]{:S(2)}, u32[]{:S(2)}) collective-permute-start(f32[1,48,48,6]{2,1,3,0:T(8,128)} %copy.45), channel_id=1, source_target_pairs={{1,0},{0,1},{3,2},{2,3},{5,4},{4,5},{7,6},{6,7},{9,8},{8,9},{11,10... | collective-permute-start | bytes 165896 | tf_op jit(solution)/shard_map/ppermute | solution.py:33
  176.8 1.5 copy-start.11
  198.1 4.3 %copy-start.4 = (f32[1,60,54,140]{3,1,2,0:T(8,128)}, f32[1,60,54,140]{3,1,2,0:T(8,128)S(1)}, u32[]{:S(2)}) copy-start(f32[1,60,54,140]{3,1,2,0:T(8,128)S(1)} %get-tuple-element.7) | copy-start | bytes 5443204
  202.4 10.7 %copy-start.1 = (f32[4,48,12,128]{3,1,2,0:T(8,128)S(1)}, f32[4,48,12,128]{3,1,2,0:T(8,128)}, u32[]{:S(2)}) copy-start(f32[4,48,12,128]{3,1,2,0:T(8,128)} %copy-done) | copy-start | bytes 3538948
Sparse Core Ops, SparseCore 0:
  79.2 28.7 all-gather.1
where the time goes:
time: 316 us; the launch traced here: 311 us
  other arithmetic  157 us (50%)
  blocking collectives  113 us (36%)
  local copies, waits for them, and re-layouts  16.7 us (5%)
  between operations  13.9 us (4%)
  waiting for transfers between devices  5.47 us (2%)
  starting transfers between devices  4.15 us (1%)
    div x1, other arithmetic, local(): factor * (applied - CENTER * current) / HALF_WIDTH - carry_factor * previous  52.2 us
    sub x1, other arithmetic, local(): factor * (applied - CENTER * current) / HALF_WIDTH - carry_factor * previous  37.9 us
    add x6, other arithmetic, apply_operator(): partial_sum = term if partial_sum is None else partial_sum + term  35.3 us
    all_to_all x1, blocking collectives, local(): lax.all_to_all(lax.all_to_all(orbitals, 'gx', split_axis=0, concat_axis=1...  32.8 us
    all_to_all x1, blocking collectives, local(): lax.all_to_all(current, 'gy', split_axis=2, concat_axis=0, tiled=True)  32.1 us
    concatenate x8, other arithmetic, local(): padded = jnp.pad(slab, ((0, 0), (6, 6), (6, 6), (0, 0)), mode='wrap')  28.6 us
    all_to_all x1, blocking collectives, local(): lax.all_to_all(orbitals, 'gx', split_axis=0, concat_axis=1, tiled=True)  24.1 us
    all_to_all x1, blocking collectives, local(): lax.all_to_all(partly, 'gx', split_axis=1, concat_axis=0, tiled=True)  18.3 us
  transfers between devices with their start and end apart: 5, of which 2 were waited for; matrix products, arithmetic and copies ran while one was open for 11% of the time, Pallas kernels for 0%

commit v1 on v0

v1 whole, which is shorter than its diff:
```python
import functools

import jax
import jax.numpy as jnp
import numpy as np
from jax import lax
from jax.experimental import pallas as pl
from jax.experimental.pallas import tpu as pltpu
from jax.sharding import PartitionSpec as P

DEGREE = 2
SECOND = (
    -5369.0 / 1800.0,
    12.0 / 7.0,
    -15.0 / 56.0,
    10.0 / 189.0,
    -1.0 / 112.0,
    2.0 / 1925.0,
    -1.0 / 16632.0,
)
FIRST = (6.0 / 7.0, -15.0 / 56.0, 5.0 / 63.0, -1.0 / 56.0, 3.0 / 385.0, -1.0 / 792.0)
METRIC = ((1.0, 0.25, 0.15), (0.25, 1.0, 0.2), (0.15, 0.2, 1.0))
CENTER = 10.5
HALF_WIDTH = 9.5
R = 6
Y0 = 8
MESH = pl.DeviceIdType.MESH


def z_matrices(bz):
    w = np.zeros((bz + 128, 2 * bz), np.float64)

    def row(p):
        return p if 0 <= p < bz else (bz + 8 + p if p < 0 else p + 8)

    for n in range(bz):
        for k in range(1, R + 1):
            w[row(n + k), n] += FIRST[k - 1]
            w[row(n - k), n] -= FIRST[k - 1]
            w[row(n + k), bz + n] += -0.5 * METRIC[2][2] * SECOND[k]
            w[row(n - k), bz + n] += -0.5 * METRIC[2][2] * SECOND[k]
    high = w.astype(np.float32).astype(jnp.bfloat16)
    low = (w - high.astype(np.float64)).astype(np.float32).astype(jnp.bfloat16)
    return jnp.asarray(high), jnp.asarray(low)


def kernel(
    gx, gy, gz,
    orb, pot, whi_ref, wlo_ref, out,
    vin, pin, v0, v1, a_ref, c_ref, s_ref, obuf, ebuf, hbuf,
    isend, irecv, psend, precv, qsend, qrecv, hsend, hrecv, osend, orecv, lsem,
):
    _, bx, by, bz = orb.shape
    nx, ny = gx * bx, gy * by
    cx, cy, cz = lax.axis_index("gx"), lax.axis_index("gy"), lax.axis_index("gz")
    band = cx * gy + cy
    zl, zr = lax.rem(cz + gz - 1, gz), lax.rem(cz + 1, gz)
    peers = [(dx, dy) for dx in range(gx) for dy in range(gy) if dx or dy]
    order = sorted(peers, key=lambda d: -min(d[1], gy - d[1]))

    def there(dx, dy):
        return lax.rem(cx + dx, gx), lax.rem(cy + dy, gy)

    barrier = pltpu.get_barrier_semaphore()
    for dx, dy in peers:
        tx, ty = there(dx, dy)
        pl.semaphore_signal(barrier, inc=1, device_id=(tx, ty, cz), device_id_type=MESH)
    for z in (zl, zr):
        pl.semaphore_signal(barrier, inc=1, device_id=(cx, cy, z), device_id_type=MESH)
    pl.semaphore_wait(barrier, len(peers) + 2)

    own = pltpu.make_async_copy(orb.at[band], vin.at[cx, cy], lsem.at[0])
    own.start()
    own_pot = pltpu.make_async_copy(pot, pin.at[cx, cy], lsem.at[1])
    own_pot.start()
    incoming = []
    for dx, dy in order:
        tx, ty = there(dx, dy)
        i = dx * gy + dy
        copy = pltpu.make_async_remote_copy(
            orb.at[tx * gy + ty], vin.at[cx, cy], isend.at[i], irecv.at[i],
            device_id=(tx, ty, cz), device_id_type=MESH,
        )
        copy.start()
        incoming.append(copy)
    gathers = []
    for dy in range(1, gy):
        copy = pltpu.make_async_remote_copy(
            pot, pin.at[cx, cy], psend.at[dy], precv.at[dy],
            device_id=(cx, lax.rem(cy + dy, gy), cz), device_id_type=MESH,
        )
        copy.start()
        gathers.append(copy)
    own.wait()
    for copy in incoming:
        copy.wait()

    def wrap_y(ref, x):
        ref[x, pl.ds(Y0 - R, R), :] = ref[x, pl.ds(Y0 + ny - R, R), :]
        ref[x, pl.ds(Y0 + ny, R), :] = ref[x, pl.ds(Y0, R), :]

    def wrap_x(ref):
        ref[pl.ds(0, R)] = ref[pl.ds(nx, R)]
        ref[pl.ds(nx + R, R)] = ref[pl.ds(R, R)]

    for sx in range(gx):
        @pl.loop(0, bx)
        def _(i):
            x = sx * bx + i + R
            for sy in range(gy):
                v0[x, pl.ds(Y0 + sy * by, by), :] = vin[sx, sy, i]
            wrap_y(v0, x)
    wrap_x(v0)

    xc = 8
    rows = xc * ny
    blocks = rows // 128

    def send_edges(step, v):
        @pl.loop(0, nx // xc)
        def _(c):
            vals = v[pl.ds(c * xc + R, xc), pl.ds(Y0, ny), :].reshape(rows, bz)
            for i in range(blocks):
                at = pl.multiple_of(c * rows + i * 128, 128)
                t = vals[i * 128 : (i + 1) * 128].T
                ebuf[step, 0, :, pl.ds(at, 128)] = t[:8]
                ebuf[step, 1, :, pl.ds(at, 128)] = t[bz - 8 :]

        copies = []
        for side, z in ((0, zl), (1, zr)):
            copy = pltpu.make_async_remote_copy(
                ebuf.at[step, side], hbuf.at[step, 1 - side],
                hsend.at[step, side], hrecv.at[step, 1 - side],
                device_id=(cx, cy, z), device_id_type=MESH,
            )
            copy.start()
            copies.append(copy)
        return copies

    def y_pass(v):
        @pl.loop(0, nx)
        def _(x):
            first = second = None
            for k in range(1, R + 1):
                up = v[x + R, pl.ds(Y0 + k, ny), :]
                down = v[x + R, pl.ds(Y0 - k, ny), :]
                f = (-METRIC[0][1] * FIRST[k - 1]) * (up - down)
                s = (-0.5 * METRIC[1][1] * SECOND[k]) * (up + down)
                first = f if first is None else first + f
                second = s if second is None else second + s
            c_ref[x + R] = first
            s_ref[x] = second

    def z_pass(step, v):
        @pl.loop(0, nx // xc)
        def _(c):
            vals = v[pl.ds(c * xc + R, xc), pl.ds(Y0, ny), :].reshape(rows, bz)
            sides = []
            for i in range(blocks):
                at = pl.multiple_of(c * rows + i * 128, 128)
                block = jnp.concatenate(
                    [
                        hbuf[step, 0, :, pl.ds(at, 128)],
                        hbuf[step, 1, :, pl.ds(at, 128)],
                        jnp.zeros((112, 128), jnp.float32),
                    ],
                    axis=0,
                )
                sides.append(block.T)
            full = jnp.concatenate([vals, jnp.concatenate(sides, axis=0)], axis=1)
            high = full.astype(jnp.bfloat16)
            low = (full - high.astype(jnp.float32)).astype(jnp.bfloat16)
            dot = functools.partial(jnp.dot, preferred_element_type=jnp.float32)
            whi = whi_ref[...]
            got = dot(high, whi) + (dot(low, whi) + dot(high, wlo_ref[...]))
            a = got[:, :bz].reshape(xc, ny, bz)
            s_ref[pl.ds(c * xc, xc)] += got[:, bz:].reshape(xc, ny, bz)
            c_ref[pl.ds(c * xc + R, xc)] += (-METRIC[0][2]) * a
            a_ref[pl.ds(c * xc, xc), pl.ds(Y0, ny), :] = a
            for i in range(xc):
                wrap_y(a_ref, c * xc + i)

        wrap_x(c_ref)

    def x_row(v, x, sx, i):
        centre = v[x + R, pl.ds(Y0, ny), :]
        local_pot = jnp.concatenate([pin[sx, sy, i] for sy in range(gy)], axis=0)
        total = s_ref[x] + (local_pot + (-1.5 * SECOND[0] - CENTER)) * centre
        for k in range(1, R + 1):
            total = total + (-0.5 * METRIC[0][0] * SECOND[k]) * (
                v[x + R + k, pl.ds(Y0, ny), :] + v[x + R - k, pl.ds(Y0, ny), :]
            )
            total = total + FIRST[k - 1] * (c_ref[x + R + k] - c_ref[x + R - k])
            total = total + (-METRIC[1][2] * FIRST[k - 1]) * (
                a_ref[x, pl.ds(Y0 + k, ny), :] - a_ref[x, pl.ds(Y0 - k, ny), :]
            )
        return total

    edges = send_edges(0, v0)
    y_pass(v0)
    own_pot.wait()
    for copy in gathers:
        copy.wait()
    spread = []
    for dx in range(1, gx):
        copy = pltpu.make_async_remote_copy(
            pin.at[cx], pin.at[cx], qsend.at[dx], qrecv.at[dx],
            device_id=(lax.rem(cx + dx, gx), cy, cz), device_id_type=MESH,
        )
        copy.start()
        spread.append(copy)
    for copy in edges:
        copy.wait()
    z_pass(0, v0)
    for copy in spread:
        copy.wait()
    for sx in range(gx):
        @pl.loop(0, bx)
        def _(i):
            x = sx * bx + i
            v1[x + R, pl.ds(Y0, ny), :] = (1.0 / HALF_WIDTH) * x_row(v0, x, sx, i)
            wrap_y(v1, x + R)
    wrap_x(v1)

    edges = send_edges(1, v1)
    y_pass(v1)
    for copy in edges:
        copy.wait()
    z_pass(1, v1)
    outgoing = []
    for dx in list(range(1, gx)) + [0]:
        tx = lax.rem(cx + dx, gx)

        @pl.loop(0, bx)
        def _(i):
            x = tx * bx + i
            got = (2.0 / HALF_WIDTH) * x_row(v1, x, tx, i) - v0[x + R, pl.ds(Y0, ny), :]
            for sy in range(gy):
                obuf[tx, sy, i] = got[sy * by : (sy + 1) * by]

        for dy in sorted(range(gy), key=lambda d: -min(d, gy - d)):
            ty = lax.rem(cy + dy, gy)
            n = dx * gy + dy
            if n == 0:
                copy = pltpu.make_async_copy(obuf.at[tx, ty], out.at[band], lsem.at[2])
            else:
                copy = pltpu.make_async_remote_copy(
                    obuf.at[tx, ty], out.at[band], osend.at[n], orecv.at[n],
                    device_id=(tx, ty, cz), device_id_type=MESH,
                )
            copy.start()
            outgoing.append(copy)
    for copy in outgoing:
        copy.wait()


def local(sizes, orbitals, potential):
    gx, gy, gz = sizes
    bands, bx, by, bz = orbitals.shape
    nx, ny = gx * bx, gy * by
    assert bands == gx * gy and gz > 1
    f32 = jnp.float32
    whi, wlo = z_matrices(bz)
    anywhere = pl.BlockSpec(memory_space=pl.ANY)
    vmem = pl.BlockSpec(memory_space=pltpu.VMEM)
    dma = pltpu.SemaphoreType.DMA
    return pl.pallas_call(
        functools.partial(kernel, gx, gy, gz),
        out_shape=jax.ShapeDtypeStruct(orbitals.shape, f32),
        in_specs=[anywhere, anywhere, vmem, vmem],
        out_specs=anywhere,
        scratch_shapes=[
            pltpu.VMEM((gx, gy, bx, by, bz), f32),
            pltpu.VMEM((gx, gy, bx, by, bz), f32),
            pltpu.VMEM((nx + 2 * R, ny + 16, bz), f32),
            pltpu.VMEM((nx + 2 * R, ny + 16, bz), f32),
            pltpu.VMEM((nx, ny + 16, bz), f32),
            pltpu.VMEM((nx + 2 * R, ny, bz), f32),
            pltpu.VMEM((nx, ny, bz), f32),
            pltpu.VMEM((gx, gy, bx, by, bz), f32),
            pltpu.VMEM((DEGREE, 2, 8, nx * ny), f32),
            pltpu.VMEM((DEGREE, 2, 8, nx * ny), f32),
            dma((gx * gy,)), dma((gx * gy,)),
            dma((gy,)), dma((gy,)),
            dma((gx,)), dma((gx,)),
            dma((DEGREE, 2)), dma((DEGREE, 2)),
            dma((gx * gy,)), dma((gx * gy,)),
            dma((3,)),
        ],
        compiler_params=pltpu.CompilerParams(
            collective_id=0, has_side_effects=True, vmem_limit_bytes=48 * 1024 * 1024
        ),
    )(orbitals, potential, whi, wlo)


def solution(mesh):
    sizes = tuple(mesh.shape[a] for a in ("gx", "gy", "gz"))
    return jax.shard_map(
        functools.partial(local, sizes),
        mesh=mesh,
        in_specs=(P(None, "gx", "gy", "gz"), P("gx", "gy", "gz")),
        out_specs=P(None, "gx", "gy", "gz"),
        check_vma=False,
    )
```

time: 316 us -> 95.8 us (0.30); the launches traced: 311 us -> 95.7 us
  other arithmetic: 157 us -> 0 us
  blocking collectives: 113 us -> 0 us
  Pallas kernels: 0 us -> 92.2 us
  between operations: 13.9 us -> 0.04 us
  local copies, waits for them, and re-layouts: 16.7 us -> 3.43 us
  waiting for transfers between devices: 5.47 us -> 0 us
  starting transfers between devices: 4.15 us -> 0 us
    all_to_all x4 -> x0, blocking collectives: 107 us -> none  [the longest x1 32.8 us: local(): lax.all_to_all(lax.all_to_all(orbitals, 'gx', split_axis=0, concat_axis=1...]
    pallas_call x0 -> x1, Pallas kernels: none -> 92.2 us  [local(): pl.pallas_call(functools.partial(kernel, gx, gy, gz), out_shape=jax.Shape...]
    div x1 -> x0, other arithmetic: 52.2 us -> none  [local(): factor * (applied - CENTER * current) / HALF_WIDTH - carry_factor * previous]
    sub x1 -> x0, other arithmetic: 37.9 us -> none  [local(): factor * (applied - CENTER * current) / HALF_WIDTH - carry_factor * previous]
    add x6 -> x0, other arithmetic: 35.3 us -> none  [apply_operator(): partial_sum = term if partial_sum is None else partial_sum + term]
    concatenate x10 -> x0, other arithmetic: 31.5 us -> none  [the longest x8 28.6 us: local(): padded = jnp.pad(slab, ((0, 0), (6, 6), (6, 6), (0, 0)), mode='wrap')]
    all_gather x1 -> x0, blocking collectives: 6.13 us -> none  [local(): plane_x = lax.all_gather(potential, 'gx', axis=0, tiled=True)]
    slice x8 -> x0, local copies, waits for them, and re-layouts: 5.96 us -> none  [the longest x4 4.12 us: extended(): lax.slice_in_dim(block, block.shape[dim] - width, None, axis=dim)]
  transfers between devices with their start and end apart: 5 -> 0, of which waited for: 2 -> 0; matrix products, arithmetic and copies ran while one was open for 11% -> 0% of each run, Pallas kernels for 0% -> 0%
where the time goes in v1:
time: 95.8 us; the launch traced here: 95.7 us
  Pallas kernels  92.2 us (96%)
  local copies, waits for them, and re-layouts  3.43 us (4%)
    pallas_call x1, Pallas kernels, local(): pl.pallas_call(functools.partial(kernel, gx, gy, gz), out_shape=jax.Shape...  92.2 us

profile of v1, /device:TPU:0, one launch (start us, length us, event | category | flops | bytes accessed | tf_op | source)
XLA Modules:
  0.0 95.7 jit_solution(14589378454130949018)
XLA Ops:
  0.0 0.0 copy-start
  0.0 0.0 copy-start.1
  0.0 0.0 copy-start.2
  0.0 1.7 %copy.5.orb = f32[16,12,12,128]{3,2,1,0:T(8,128)S(1)} copy(f32[16,12,12,128]{3,0,2,1:T(8,128)} %param.4) | data formatting | bytes 2359296 | tf_op args[0]
  1.7 0.0 copy-done
  1.7 0.0 copy-done.1
  1.8 0.0 copy-done.2
  1.8 92.2 %shard_map.46 = f32[16,12,12,128]{3,2,1,0:T(8,128)S(1)} custom-call(f32[16,12,12,128]{3,2,1,0:T(8,128)S(1)} %copy.5.orb, f32[12,12,128]{2,1,0:T(8,128)S(1)} %copy-done.2, bf16[256,256]{1,0:T(8,128)(2,1)S(1)} %copy-done.1, bf16[256,256]{1,0:T(8,128)(2,1)S(1)} %copy-done), custom_call_target="tpu_custom_call" | custom-call | tf_op jit(solution)/shard_map/pallas_call | solution.py:267
  94.0 1.7 %copy.6 = f32[16,12,12,128]{3,0,2,1:T(8,128)} copy(f32[16,12,12,128]{3,2,1,0:T(8,128)S(1)} %shard_map.46) | data formatting | bytes 2359296 | tf_op jit(solution)/shard_map/pallas_call | solution.py:267
Async XLA Ops:
  0.0 1.7 %copy-start = (bf16[256,256]{1,0:T(8,128)(2,1)S(1)}, bf16[256,256]{1,0:T(8,128)(2,1)}, u32[]{:S(2)}) copy-start(bf16[256,256]{1,0:T(8,128)(2,1)} %constant.5.clone.wlo_ref) | copy-start | bytes 393220
  0.0 1.7 %copy-start.1 = (bf16[256,256]{1,0:T(8,128)(2,1)S(1)}, bf16[256,256]{1,0:T(8,128)(2,1)}, u32[]{:S(2)}) copy-start(bf16[256,256]{1,0:T(8,128)(2,1)} %constant.4.clone.whi_ref) | copy-start | bytes 393220
  0.0 1.8 %copy-start.2 = (f32[12,12,128]{2,1,0:T(8,128)S(1)}, f32[12,12,128]{2,1,0:T(8,128)}, u32[]{:S(2)}) copy-start(f32[12,12,128]{2,1,0:T(8,128)} %pot.1) | copy-start | bytes 221188

commit v2 on v1

v2 whole, which is shorter than its diff:
```python
import functools
import math

import jax
import jax.numpy as jnp
import numpy as np
from jax import lax
from jax.experimental import pallas as pl
from jax.experimental.pallas import tpu as pltpu
from jax.sharding import PartitionSpec as P

DEGREE = 2
SECOND = (
    -5369.0 / 1800.0,
    12.0 / 7.0,
    -15.0 / 56.0,
    10.0 / 189.0,
    -1.0 / 112.0,
    2.0 / 1925.0,
    -1.0 / 16632.0,
)
FIRST = (6.0 / 7.0, -15.0 / 56.0, 5.0 / 63.0, -1.0 / 56.0, 3.0 / 385.0, -1.0 / 792.0)
METRIC = ((1.0, 0.25, 0.15), (0.25, 1.0, 0.2), (0.15, 0.2, 1.0))
CENTER = 10.5
HALF_WIDTH = 9.5
R = 6
Y0 = 8
MESH = pl.DeviceIdType.MESH


def z_matrices(bz):
    w = np.zeros((bz + 128, 2 * bz), np.float64)

    def row(p):
        return p if 0 <= p < bz else (bz + 8 + p if p < 0 else p + 8)

    for n in range(bz):
        for k in range(1, R + 1):
            w[row(n + k), n] += FIRST[k - 1]
            w[row(n - k), n] -= FIRST[k - 1]
            w[row(n + k), bz + n] += -0.5 * METRIC[2][2] * SECOND[k]
            w[row(n - k), bz + n] += -0.5 * METRIC[2][2] * SECOND[k]
    high = w.astype(np.float32).astype(jnp.bfloat16)
    low = (w - high.astype(np.float64)).astype(np.float32).astype(jnp.bfloat16)
    return jnp.asarray(high), jnp.asarray(low)


def kernel(
    gx, gy, gz, bx, by,
    orb, pot, whi_ref, wlo_ref, out,
    vin, pin, p_ref, v0, v1, a_ref, c0, c1, s_ref, obuf, ebuf, hbuf,
    isend, irecv, psend, precv, qsend, qrecv, hsend, hrecv, osend, orecv, lsem,
):
    bz = orb.shape[-1]
    nx, ny = gx * bx, gy * by
    group = 8 // math.gcd(by, 8)
    rows = bx * ny
    padded_rows = ebuf.shape[-1]
    cx, cy, cz = lax.axis_index("gx"), lax.axis_index("gy"), lax.axis_index("gz")
    band = cx * gy + cy
    zl, zr = lax.rem(cz + gz - 1, gz), lax.rem(cz + 1, gz)
    far_first = sorted(range(1, gy), key=lambda d: -min(d, gy - d))

    barrier = pltpu.get_barrier_semaphore()
    for dx in range(gx):
        for dy in range(gy):
            if dx or dy:
                pl.semaphore_signal(
                    barrier, inc=1,
                    device_id=(lax.rem(cx + dx, gx), lax.rem(cy + dy, gy), cz),
                    device_id_type=MESH,
                )
    for z in (zl, zr):
        pl.semaphore_signal(barrier, inc=1, device_id=(cx, cy, z), device_id_type=MESH)
    pl.semaphore_wait(barrier, gx * gy + 1)

    own_pot = pltpu.make_async_copy(pot, pin.at[cx, cy], lsem.at[1])
    own_pot.start()
    gathers = [own_pot]
    for dy in far_first:
        copy = pltpu.make_async_remote_copy(
            pot, pin.at[cx, cy], psend.at[dy], precv.at[dy],
            device_id=(cx, lax.rem(cy + dy, gy), cz), device_id_type=MESH,
        )
        copy.start()
        gathers.append(copy)

    def send_bands(dx):
        tx = lax.rem(cx + dx, gx)
        copies = []
        for dy in far_first + [0]:
            ty = lax.rem(cy + dy, gy)
            n = dx * gy + dy
            if n == 0:
                copy = pltpu.make_async_copy(orb.at[band], vin.at[cx, cy], lsem.at[0])
            else:
                copy = pltpu.make_async_remote_copy(
                    orb.at[tx * gy + ty], vin.at[cx, cy], isend.at[n], irecv.at[n],
                    device_id=(tx, ty, cz), device_id_type=MESH,
                )
            copy.start()
            copies.append(copy)
        return copies

    spread_steps = []
    d = gx // 2
    while d:
        spread_steps.append(d)
        d //= 2
    held = [cx]
    spread_count = [0]

    def spread(d):
        bit = lax.rem(lax.div(cx, d), 2)
        hop = d - 2 * d * bit
        copies = []
        for r in list(held):
            i = spread_count[0]
            spread_count[0] += 1
            copy = pltpu.make_async_remote_copy(
                pin.at[r], pin.at[r], qsend.at[i], qrecv.at[i],
                device_id=(cx + hop, cy, cz), device_id_type=MESH,
            )
            copy.start()
            copies.append(copy)
            held.append(r + hop)
        return copies

    def wrap_y(ref, x):
        ref[x, pl.ds(Y0 - R, R), :] = ref[x, pl.ds(Y0 + ny - R, R), :]
        ref[x, pl.ds(Y0 + ny, R), :] = ref[x, pl.ds(Y0, R), :]

    def wrap_x(ref, sx):
        @pl.when(sx == 0)
        def _():
            ref[pl.ds(nx + R, R)] = ref[pl.ds(R, R)]

        @pl.when(sx == gx - 1)
        def _():
            ref[pl.ds(0, R)] = ref[pl.ds(nx, R)]

    def pieces(ref, sx, i):
        at = pl.multiple_of(i * group * by, 8)
        for sy in range(gy):
            got = ref[sx, sy, pl.ds(at, group * by), :]
            for j in range(group):
                yield sy, j, got[j * by : (j + 1) * by]

    def assemble(sx):
        @pl.loop(0, bx // group)
        def _(i):
            x = sx * bx + i * group + R
            for sy, j, piece in pieces(vin, sx, i):
                v0[x + j, pl.ds(Y0 + sy * by, by), :] = piece
            for j in range(group):
                wrap_y(v0, x + j)
        wrap_x(v0, sx)

    def assemble_potential():
        for sx in range(gx):
            @pl.loop(0, bx // group)
            def _(i):
                x = sx * bx + i * group
                for sy, j, piece in pieces(pin, sx, i):
                    p_ref[x + j, pl.ds(sy * by, by), :] = piece + (-1.5 * SECOND[0] - CENTER)

    def send_edges(step, v, sx, t):
        vals = v[pl.ds(sx * bx + R, bx), pl.ds(Y0, ny), :].reshape(rows, bz)
        if padded_rows > rows:
            vals = jnp.concatenate([vals, jnp.zeros((padded_rows - rows, bz), jnp.float32)], axis=0)
        for i in range(padded_rows // 128):
            turned = vals[i * 128 : (i + 1) * 128].T
            ebuf[step, t, 0, :, pl.ds(i * 128, 128)] = turned[:8]
            ebuf[step, t, 1, :, pl.ds(i * 128, 128)] = turned[bz - 8 :]
        copies = []
        for side, z in ((0, zl), (1, zr)):
            copy = pltpu.make_async_remote_copy(
                ebuf.at[step, t, side], hbuf.at[step, t, 1 - side],
                hsend.at[step, t, side], hrecv.at[step, t, 1 - side],
                device_id=(cx, cy, z), device_id_type=MESH,
            )
            copy.start()
            copies.append(copy)
        return copies

    def y_pass(v, c_ref, sx):
        @pl.loop(0, bx)
        def _(i):
            x = sx * bx + i
            first = second = None
            for k in range(1, R + 1):
                up = v[x + R, pl.ds(Y0 + k, ny), :]
                down = v[x + R, pl.ds(Y0 - k, ny), :]
                f = (-METRIC[0][1] * FIRST[k - 1]) * (up - down)
                s = (-0.5 * METRIC[1][1] * SECOND[k]) * (up + down)
                first = f if first is None else first + f
                second = s if second is None else second + s
            c_ref[x + R] = first
            s_ref[x] = second

    def z_pass(step, v, c_ref, sx, t):
        vals = v[pl.ds(sx * bx + R, bx), pl.ds(Y0, ny), :].reshape(rows, bz)
        sides = []
        for i in range(padded_rows // 128):
            block = jnp.concatenate(
                [
                    hbuf[step, t, 0, :, pl.ds(i * 128, 128)],
                    hbuf[step, t, 1, :, pl.ds(i * 128, 128)],
                    jnp.zeros((112, 128), jnp.float32),
                ],
                axis=0,
            )
            sides.append(block.T)
        full = jnp.concatenate([vals, jnp.concatenate(sides, axis=0)[:rows]], axis=1)
        high = full.astype(jnp.bfloat16)
        low = (full - high.astype(jnp.float32)).astype(jnp.bfloat16)
        dot = functools.partial(jnp.dot, preferred_element_type=jnp.float32)
        whi = whi_ref[...]
        got = dot(high, whi) + (dot(low, whi) + dot(high, wlo_ref[...]))
        a = got[:, :bz].reshape(bx, ny, bz)
        s_ref[pl.ds(sx * bx, bx)] += got[:, bz:].reshape(bx, ny, bz)
        c_ref[pl.ds(sx * bx + R, bx)] += (-METRIC[0][2]) * a
        a_ref[pl.ds(sx * bx, bx), pl.ds(Y0, ny), :] = a
        for i in range(bx):
            wrap_y(a_ref, sx * bx + i)
        wrap_x(c_ref, sx)

    def x_row(v, c_ref, x):
        total = s_ref[x] + p_ref[x] * v[x + R, pl.ds(Y0, ny), :]
        for k in range(1, R + 1):
            total = total + (-0.5 * METRIC[0][0] * SECOND[k]) * (
                v[x + R + k, pl.ds(Y0, ny), :] + v[x + R - k, pl.ds(Y0, ny), :]
            )
            total = total + FIRST[k - 1] * (c_ref[x + R + k] - c_ref[x + R - k])
            total = total + (-METRIC[1][2] * FIRST[k - 1]) * (
                a_ref[x, pl.ds(Y0 + k, ny), :] - a_ref[x, pl.ds(Y0 - k, ny), :]
            )
        return total

    def wait_all(copies):
        for copy in copies:
            copy.wait()

    block = [lax.rem(cx + gx - t, gx) for t in range(gx)]
    second_edges = {}

    def first_x_pass(t):
        sx = block[t]

        @pl.loop(0, bx)
        def _(i):
            x = sx * bx + i
            v1[x + R, pl.ds(Y0, ny), :] = (1.0 / HALF_WIDTH) * x_row(v0, c0, x)
            wrap_y(v1, x + R)
        wrap_x(v1, sx)
        second_edges[t] = send_edges(1, v1, sx, t)
        y_pass(v1, c1, sx)

    half = (gx + 1) // 2
    bands_in = [send_bands(dx) for dx in range(half)]
    wait_all(gathers)
    doing = spread(spread_steps[0])
    bands_in += [send_bands(dx) for dx in range(half, gx)]
    first_edges = []
    for t in range(gx):
        wait_all(bands_in[t])
        assemble(block[t])
        first_edges.append(send_edges(0, v0, block[t], t))
        y_pass(v0, c0, block[t])
        if 1 <= t < gx - 1:
            wait_all(doing)
            doing = spread(spread_steps[t]) if t < len(spread_steps) else []
        if t == gx - 1:
            wait_all(doing)
            assemble_potential()
        if t >= 1:
            wait_all(first_edges[t - 1])
            z_pass(0, v0, c0, block[t - 1], t - 1)
    for t in range(1, gx - 2):
        first_x_pass(t)
    wait_all(first_edges[gx - 1])
    z_pass(0, v0, c0, block[gx - 1], gx - 1)
    late = [gx - 2, gx - 1, 0]
    for t in late:
        first_x_pass(t)

    outgoing = []

    def last_x_pass(t):
        sx = block[t]

        @pl.loop(0, bx // group)
        def _(i):
            got = []
            for j in range(group):
                x = sx * bx + i * group + j
                got.append(
                    (2.0 / HALF_WIDTH) * x_row(v1, c1, x) - v0[x + R, pl.ds(Y0, ny), :]
                )
            at = pl.multiple_of(i * group * by, 8)
            for sy in range(gy):
                obuf[sx, sy, pl.ds(at, group * by), :] = jnp.concatenate(
                    [g[sy * by : (sy + 1) * by] for g in got], axis=0
                )

        for dy in far_first + [0]:
            ty = lax.rem(cy + dy, gy)
            n = t * gy + dy
            if n == 0:
                copy = pltpu.make_async_copy(obuf.at[sx, ty], out.at[band], lsem.at[2])
            else:
                copy = pltpu.make_async_remote_copy(
                    obuf.at[sx, ty], out.at[band], osend.at[n], orecv.at[n],
                    device_id=(sx, ty, cz), device_id_type=MESH,
                )
            copy.start()
            outgoing.append(copy)

    ready = list(range(1, gx - 2)) + late
    done = []
    for t in ready:
        wait_all(second_edges[t])
        z_pass(1, v1, c1, block[t], t)
        done.append(t)
        for u in range(gx):
            near = {u, (u + 1) % gx, (u - 1) % gx}
            if near <= set(done) and t in near:
                last_x_pass(u)
    wait_all(outgoing)


def local(sizes, orbitals, potential):
    gx, gy, gz = sizes
    bands, bx, by, bz = orbitals.shape
    nx, ny = gx * bx, gy * by
    assert bands == gx * gy and gz > 1 and gx >= 4 and gx & (gx - 1) == 0
    f32 = jnp.float32
    whi, wlo = z_matrices(bz)
    anywhere = pl.BlockSpec(memory_space=pl.ANY)
    vmem = pl.BlockSpec(memory_space=pltpu.VMEM)
    dma = pltpu.SemaphoreType.DMA
    edge = (DEGREE, gx, 2, 8, (bx * ny + 127) // 128 * 128)
    out = pl.pallas_call(
        functools.partial(kernel, gx, gy, gz, bx, by),
        out_shape=jax.ShapeDtypeStruct((bands, bx * by, bz), f32),
        in_specs=[anywhere, anywhere, vmem, vmem],
        out_specs=anywhere,
        scratch_shapes=[
            pltpu.VMEM((gx, gy, bx * by, bz), f32),
            pltpu.VMEM((gx, gy, bx * by, bz), f32),
            pltpu.VMEM((nx, ny, bz), f32),
            pltpu.VMEM((nx + 2 * R, ny + 16, bz), f32),
            pltpu.VMEM((nx + 2 * R, ny + 16, bz), f32),
            pltpu.VMEM((nx, ny + 16, bz), f32),
            pltpu.VMEM((nx + 2 * R, ny, bz), f32),
            pltpu.VMEM((nx + 2 * R, ny, bz), f32),
            pltpu.VMEM((nx, ny, bz), f32),
            pltpu.VMEM((gx, gy, bx * by, bz), f32),
            pltpu.VMEM(edge, f32),
            pltpu.VMEM(edge, f32),
            dma((gx * gy,)), dma((gx * gy,)),
            dma((gy,)), dma((gy,)),
            dma((gx,)), dma((gx,)),
            dma((DEGREE, gx, 2)), dma((DEGREE, gx, 2)),
            dma((gx * gy,)), dma((gx * gy,)),
            dma((3,)),
        ],
        compiler_params=pltpu.CompilerParams(
            collective_id=0, has_side_effects=True, vmem_limit_bytes=48 * 1024 * 1024
        ),
    )(
        orbitals.reshape(bands, bx * by, bz),
        potential.reshape(bx * by, bz),
        whi,
        wlo,
    )
    return out.reshape(bands, bx, by, bz)


def solution(mesh):
    sizes = tuple(mesh.shape[a] for a in ("gx", "gy", "gz"))
    return jax.shard_map(
        functools.partial(local, sizes),
        mesh=mesh,
        in_specs=(P(None, "gx", "gy", "gz"), P("gx", "gy", "gz")),
        out_specs=P(None, "gx", "gy", "gz"),
        check_vma=False,
    )
```

time: 95.8 us -> 81.3 us (0.85)
  Pallas kernels: 92.2 us -> 77.1 us
    pallas_call x1, Pallas kernels: 92.2 us -> 77.1 us  [local(): pl.pallas_call(functools.partial(kernel, gx, gy, gz, bx, by), out_shape=j...]
    reshape x0 -> x2, local copies, waits for them, and re-layouts: none -> 2.59 us  [the longest x1 1.7 us: local(): orbitals.reshape(bands, bx * by, bz)]
    unnamed x7 -> x4, local copies, waits for them, and re-layouts: 1.73 us -> 0.01 us
where the time goes in v2:
time: 81.3 us; the launch traced here: 81.1 us
  Pallas kernels  77.1 us (95%)
  local copies, waits for them, and re-layouts  3.98 us (5%)
    pallas_call x1, Pallas kernels, local(): pl.pallas_call(functools.partial(kernel, gx, gy, gz, bx, by), out_shape=j...  77.1 us
    reshape x1, local copies, waits for them, and re-layouts, local(): orbitals.reshape(bands, bx * by, bz)  1.7 us

profile of v2, /device:TPU:0, one launch (start us, length us, event | category | flops | bytes accessed | tf_op | source)
XLA Modules:
  0.0 81.1 jit_solution(7601480268721228090)
XLA Ops:
  0.0 0.9 %reshape.10.pot = f32[144,128]{1,0:T(8,128)S(1)} reshape(f32[12,12,128]{2,1,0:T(8,128)} %param.5) | data formatting | bytes 147456 | tf_op jit(solution)/shard_map/reshape | solution.py:373
  0.9 0.0 copy-start
  0.9 0.0 copy-start.1
  0.9 1.7 %copy.7.orb = f32[16,144,128]{2,1,0:T(8,128)S(1)} copy(f32[16,144,128]{2,0,1:T(8,128)} %bitcast.2) | data formatting | bytes 2359296 | tf_op jit(solution)/shard_map/reshape | solution.py:372
  2.6 0.0 copy-done
  2.6 0.0 copy-done.1
  2.6 77.1 %shard_map.46 = f32[16,144,128]{2,1,0:T(8,128)S(1)} custom-call(f32[16,144,128]{2,1,0:T(8,128)S(1)} %copy.7.orb, f32[144,128]{1,0:T(8,128)S(1)} %reshape.10.pot, bf16[256,256]{1,0:T(8,128)(2,1)S(1)} %copy-done.1, bf16[256,256]{1,0:T(8,128)(2,1)S(1)} %copy-done), custom_call_target="tpu_custom_call" | custom-call | tf_op jit(solution)/shard_map/pallas_call | solution.py:343
  79.8 1.4 %copy.8 = f32[16,144,128]{2,0,1:T(8,128)} copy(f32[16,144,128]{2,1,0:T(8,128)S(1)} %shard_map.46) | data formatting | bytes 2359296 | tf_op jit(solution)/shard_map/pallas_call | solution.py:343
Async XLA Ops:
  0.9 1.7 %copy-start = (bf16[256,256]{1,0:T(8,128)(2,1)S(1)}, bf16[256,256]{1,0:T(8,128)(2,1)}, u32[]{:S(2)}) copy-start(bf16[256,256]{1,0:T(8,128)(2,1)} %constant.5.clone.wlo_ref) | copy-start | bytes 393220
  0.9 1.7 %copy-start.1 = (bf16[256,256]{1,0:T(8,128)(2,1)S(1)}, bf16[256,256]{1,0:T(8,128)(2,1)}, u32[]{:S(2)}) copy-start(bf16[256,256]{1,0:T(8,128)(2,1)} %constant.4.clone.whi_ref) | copy-start | bytes 393220
